TPU v7x, 32 devices: a whole 2x2x4 slice. The times are simulated.
32 devices in a mesh: wide: 8 (over z, x), narrow: 4 (over y, core).
Axes of the slice: x: 2, y: 2, z: 4, core: 2. Of those that a mesh axis runs over, the one named last changes fastest.
Arguments:
- cost: float32 [1024, 16384], P('wide', 'narrow'), may hold values from 0 to 2
- plan: float32 [1024, 16384], P('wide', 'narrow'), may hold values from 0 to 2
- row_mass: float32 [1024], P('wide'), may hold values from 4096 to 28672
- col_mass: float32 [16384], P('narrow'), may hold values from 256 to 1792
- row_dual: float32 [1024], P('wide'), may hold values from -3 to 3
- col_dual: float32 [16384], P('narrow'), may hold values from -3 to 3
Outputs:
- plan_out: float32 [1024, 16384], P('wide', 'narrow')
- row_out: float32 [1024], P('wide')
- col_out: float32 [16384], P('narrow')
All inputs are finite; a program needn't handle non-finite values.
Results may differ from a plain program's by a relative error of at most 0.0001.
Values sent between devices are 32-bit elements; how exact they have to be, the bound alone decides.
A program may use at most 64 MiB of HBM per device.

v0:
```python
import math
import jax
import jax.numpy as jnp
from jax import lax
from jax.sharding import PartitionSpec as P

ITERS = 4


def shards(cost, plan, row_mass, col_mass, row_dual, col_dual):
    wide_count = lax.axis_size("wide")
    narrow_count = lax.axis_size("narrow")
    total_rows = plan.shape[0] * wide_count
    total_cols = plan.shape[1] * narrow_count
    step_base = 0.9 / math.sqrt(total_rows + total_cols)
    weight = jnp.float32(step_base)
    for step in range(ITERS):
        primal_step = step_base / weight
        dual_step = step_base * weight
        fresh = jnp.maximum(
            plan - primal_step * (cost - row_dual[:, None] - col_dual[None, :]), 0.0
        )
        change = fresh - plan
        extrap = fresh + change
        moved = jnp.sum(change * change)
        row_total = lax.psum(jnp.sum(extrap, axis=1), "narrow")
        new_row = row_dual + dual_step * (row_mass - row_total)
        row_square = jnp.sum((new_row - row_dual) ** 2)
        col_local = jnp.sum(extrap, axis=0)
        col_total = lax.psum(col_local, "wide")
        new_col = col_dual + dual_step * (col_mass - col_total)
        col_share = jnp.sum((new_col - col_dual) ** 2) / wide_count
        dual_share = row_square / narrow_count + col_share
        moved_all = lax.psum(moved, ("wide", "narrow"))
        dual_moved = lax.psum(dual_share, ("wide", "narrow"))
        weight = jnp.sqrt(weight * jnp.sqrt((dual_moved + 1.0) / (moved_all + 1.0)))
        plan, row_dual, col_dual = (fresh, new_row, new_col)
    return (plan, row_dual, col_dual)


def solution(mesh):
    in_specs = (
        P("wide", "narrow"),
        P("wide", "narrow"),
        P("wide"),
        P("narrow"),
        P("wide"),
        P("narrow"),
    )
    out_specs = (P("wide", "narrow"), P("wide"), P("narrow"))
    return jax.shard_map(shards, mesh=mesh, in_specs=in_specs, out_specs=out_specs, check_vma=False)
```

profile of v0, /device:TPU:0, one launch (start us, length us, event | category | flops | bytes accessed | tf_op | source)
XLA Modules:
  0.0 314.4 jit_solution(7714371782723744070)
XLA Ops:
  0.7 4.2 %multiply_reduce_fusion.2 = (f32[]{:T(128)}, f32[4096]{0:T(1024)S(1)}, f32[128]{0:T(128)S(1)}) fusion(f32[128,4096]{1,0:T(8,128)} %param.7, f32[4096]{0:T(1024)} %param.11, f32[128,4096]{1,0:T(8,128)} %param.6, f32[128]{0:T(128)} %param.10), kind=kLoop, calls=%fused_computation.6 | loop fusion | flops 5238655 | bytes 4228100 | tf_op jit(solution)/shard_map/reduce_sum | solution.py:25
  4.9 38.8 %psum.99 = f32[4096]{0:T(1024)S(1)} all-reduce(f32[4096]{0:T(1024)S(1)} %get-tuple-element.12), channel_id=1, replica_groups=mesh['wide'=8,'narrow'=4] {'wide'}, use_global_device_ids=true, to_apply=%region_4.0 | all-reduce | flops 4096 | bytes 32768 | tf_op jit(solution)/shard_map/psum | solution.py:30
  43.7 5.6 %psum.98 = f32[128]{0:T(128)S(1)} all-reduce(f32[128]{0:T(128)S(1)} %get-tuple-element.13), channel_id=1, replica_groups=mesh['wide'=8,'narrow'=4] {'narrow'}, use_global_device_ids=true, to_apply=%region_1.0 | all-reduce | flops 128 | bytes 1024 | tf_op jit(solution)/shard_map/psum | solution.py:26
  49.3 0.0 copy-done.3
  49.3 0.6 multiply_reduce_fusion.8
  50.6 0.6 multiply_reduce_fusion.5
  51.9 37.2 %all-reduce.2 = (f32[]{:T(128)}, f32[]{:T(128)}) all-reduce(f32[]{:T(128)S(6)} %add.94, f32[]{:T(128)} %get-tuple-element.11), channel_id=1, replica_groups=mesh['wide'=8,'narrow'=4] {'wide','narrow'}, use_global_device_ids=true, to_apply=%region_6.0 | all-reduce | flops 2 | bytes 16 | tf_op jit(solution)/shard_map/psum | solution.py:35
  90.5 3.7 %multiply_reduce_fusion.1 = (f32[]{:T(128)}, f32[128]{0:T(128)S(1)}, f32[4096]{0:T(1024)S(1)}) fusion(f32[4096]{0:T(1024)S(1)} %get-tuple-element.30, f32[128,4096]{1,0:T(8,128)} %param.6, f32[128]{0:T(128)S(1)} %get-tuple-element.32, f32[]{:T(128)S(6)} %div.39, f32[128,4096]{1,0:T(8,128)S(1)} %copy-done, f32[4096]{0:T(1024)S(1)} %copy-done.1, ...), kind=kLoop, calls=%fused_computation.4 | loop fusion | flops 7860095 | bytes 4245000 | tf_op jit(solution)/shard_map/reduce_sum | solution.py:25
  94.2 6.9 %psum.102 = f32[128]{0:T(128)S(1)} all-reduce(f32[128]{0:T(128)S(1)} %get-tuple-element.9), channel_id=1, replica_groups=mesh['wide'=8,'narrow'=4] {'narrow'}, use_global_device_ids=true, to_apply=%region_10.0 | all-reduce | flops 128 | bytes 1024 | tf_op jit(solution)/shard_map/psum | solution.py:26
  101.1 0.6 multiply_reduce_fusion.7
  102.4 35.6 %psum.103 = f32[4096]{0:T(1024)S(1)} all-reduce(f32[4096]{0:T(1024)S(1)} %get-tuple-element.10), channel_id=1, replica_groups=mesh['wide'=8,'narrow'=4] {'wide'}, use_global_device_ids=true, to_apply=%region_13.0 | all-reduce | flops 4096 | bytes 32768 | tf_op jit(solution)/shard_map/psum | solution.py:30
  138.0 0.6 multiply_reduce_fusion.4
  139.2 37.1 %all-reduce.1 = (f32[]{:T(128)}, f32[]{:T(128)}) all-reduce(f32[]{:T(128)S(6)} %add.100, f32[]{:T(128)} %get-tuple-element.8), channel_id=1, replica_groups=mesh['wide'=8,'narrow'=4] {'wide','narrow'}, use_global_device_ids=true, to_apply=%region_15.0 | all-reduce | flops 2 | bytes 16 | tf_op jit(solution)/shard_map/psum | solution.py:35
  177.8 4.2 %multiply_reduce_fusion = (f32[]{:T(128)}, f32[128]{0:T(128)S(1)}, f32[4096]{0:T(1024)S(1)}) fusion(f32[4096]{0:T(1024)S(1)} %get-tuple-element.26, f32[128,4096]{1,0:T(8,128)} %param.6, f32[128]{0:T(128)S(1)} %get-tuple-element.28, f32[]{:T(128)S(6)} %div.43, f32[4096]{0:T(1024)S(1)} %get-tuple-element.30, f32[128]{0:T(128)S(1)} %get-tuple-element.32, ...), kind=kLoop, calls=%fused_computation.2 | loop fusion | flops 10481535 | bytes 4261900 | tf_op jit(solution)/shard_map/reduce_sum | solution.py:25
  182.0 7.2 %psum.106 = f32[128]{0:T(128)S(1)} all-reduce(f32[128]{0:T(128)S(1)} %get-tuple-element.6), channel_id=1, replica_groups=mesh['wide'=8,'narrow'=4] {'narrow'}, use_global_device_ids=true, to_apply=%region_19.0 | all-reduce | flops 128 | bytes 1024 | tf_op jit(solution)/shard_map/psum | solution.py:26
  189.2 0.6 multiply_reduce_fusion.6
  190.5 35.3 %psum.107 = f32[4096]{0:T(1024)S(1)} all-reduce(f32[4096]{0:T(1024)S(1)} %get-tuple-element.7), channel_id=1, replica_groups=mesh['wide'=8,'narrow'=4] {'wide'}, use_global_device_ids=true, to_apply=%region_22.0 | all-reduce | flops 4096 | bytes 32768 | tf_op jit(solution)/shard_map/psum | solution.py:30
  225.8 0.6 multiply_reduce_fusion.3
  227.0 37.3 %all-reduce = (f32[]{:T(128)}, f32[]{:T(128)}) all-reduce(f32[]{:T(128)S(6)} %add.106, f32[]{:T(128)} %get-tuple-element.5), channel_id=1, replica_groups=mesh['wide'=8,'narrow'=4] {'wide','narrow'}, use_global_device_ids=true, to_apply=%region_24.0 | all-reduce | flops 2 | bytes 16 | tf_op jit(solution)/shard_map/psum | solution.py:35
  265.8 4.9 %fusion.6 = (f32[4096]{0:T(1024)S(1)}, f32[128]{0:T(128)S(1)}, f32[128,4096]{1,0:T(8,128)}) fusion(f32[4096]{0:T(1024)S(1)} %get-tuple-element.26, f32[128,4096]{1,0:T(8,128)} %param.6, f32[128]{0:T(128)S(1)} %get-tuple-element.28, f32[]{:T(128)S(6)} %div.43, f32[4096]{0:T(1024)S(1)} %get-tuple-element.30, f32[128]{0:T(128)S(1)} %get-tuple-element.32, ...), kind=kLoop, calls=%fused_computation.17 | loop fusion | flops 12054400 | bytes 6375948 | tf_op jit(solution)/shard_map/reduce_sum | solution.py:29
  270.7 36.8 %psum.111 = f32[4096]{0:T(1024)S(1)} all-reduce(f32[4096]{0:T(1024)S(1)} %get-tuple-element.3), channel_id=1, replica_groups=mesh['wide'=8,'narrow'=4] {'wide'}, use_global_device_ids=true, to_apply=%region_30.0 | all-reduce | flops 4096 | bytes 32768 | tf_op jit(solution)/shard_map/psum | solution.py:30
  307.5 0.6 multiply_add_fusion
  308.1 5.7 %psum.110 = f32[128]{0:T(128)S(1)} all-reduce(f32[128]{0:T(128)S(1)} %get-tuple-element.4), channel_id=1, replica_groups=mesh['wide'=8,'narrow'=4] {'narrow'}, use_global_device_ids=true, to_apply=%region_28.0 | all-reduce | flops 128 | bytes 1024 | tf_op jit(solution)/shard_map/psum | solution.py:26
  313.9 0.5 multiply_add_fusion.4
  (9 shorter events, 0.0 us)
Async XLA Ops:
  0.6 49.9 %copy-start.1 = (f32[4096]{0:T(1024)S(1)}, f32[4096]{0:T(1024)}, u32[]{:S(2)}) copy-start(f32[4096]{0:T(1024)} %param.11) | copy-start | bytes 49156
  0.6 48.7 %copy-start.3 = (f32[128]{0:T(128)S(1)}, f32[128]{0:T(128)}, u32[]{:S(2)}) copy-start(f32[128]{0:T(128)} %param.10) | copy-start | bytes 1540
  0.7 49.9 %copy-start.2 = (f32[4096]{0:T(1024)S(1)}, f32[4096]{0:T(1024)}, u32[]{:S(2)}) copy-start(f32[4096]{0:T(1024)} %param.9) | copy-start | bytes 49156
  0.7 48.7 %copy-start.4 = (f32[128]{0:T(128)S(1)}, f32[128]{0:T(128)}, u32[]{:S(2)}) copy-start(f32[128]{0:T(128)} %param.8) | copy-start | bytes 1540
  0.7 89.8 %copy-start = (f32[128,4096]{1,0:T(8,128)S(1)}, f32[128,4096]{1,0:T(8,128)}, u32[]{:S(2)}) copy-start(f32[128,4096]{1,0:T(8,128)} %param.7) | copy-start | bytes 6291460
where the time goes:
time: 315 us; the launch traced here: 314 us
  blocking collectives  284 us (90%)
  other arithmetic  21.7 us (7%)
  between operations  9.03 us (3%)
    psum x4, blocking collectives, shards(): col_total = lax.psum(col_local, 'wide')  147 us
    psum x3, blocking collectives, shards(): dual_moved = lax.psum(dual_share, ('wide', 'narrow'))  112 us
    psum x4, blocking collectives, shards(): row_total = lax.psum(jnp.sum(extrap, axis=1), 'narrow')  25.5 us
    reduce_sum x3, other arithmetic, shards(): moved = jnp.sum(change * change)  12.1 us

commit v1 on v0

--- a/solution.py
+++ b/solution.py
@@ -32,7 +32,13 @@
         col_share = jnp.sum((new_col - col_dual) ** 2) / wide_count
         dual_share = row_square / narrow_count + col_share
         moved_all = lax.psum(moved, ("wide", "narrow"))
-        dual_moved = lax.psum(dual_share, ("wide", "narrow"))
+
+        def open_slabs(m):
+            for idx in ("narrow", "wide"):
+                m = lax.psum(m, idx)
+            return m
+
+        dual_moved = open_slabs(dual_share)
         weight = jnp.sqrt(weight * jnp.sqrt((dual_moved + 1.0) / (moved_all + 1.0)))
         plan, row_dual, col_dual = (fresh, new_row, new_col)
     return (plan, row_dual, col_dual)

time: 315 us -> 390 us (1.24)
  blocking collectives: 284 us -> 358 us
    psum x3 -> x9, blocking collectives: 112 us -> 191 us  [the longest x3 118 us: shards(): moved_all = lax.psum(moved, ('wide', 'narrow'))]
where the time goes in v1:
time: 390 us; the launch traced here: 389 us
  blocking collectives  358 us (92%)
  other arithmetic  21.7 us (6%)
  between operations  9.06 us (2%)
    psum x4, blocking collectives, shards(): col_total = lax.psum(col_local, 'wide')  144 us
    psum x3, blocking collectives, shards(): moved_all = lax.psum(moved, ('wide', 'narrow'))  118 us
    psum x6, blocking collectives, open_slabs(): m = lax.psum(m, idx)  72.2 us
    psum x4, blocking collectives, shards(): row_total = lax.psum(jnp.sum(extrap, axis=1), 'narrow')  23.6 us
    reduce_sum x3, other arithmetic, shards(): moved = jnp.sum(change * change)  12.1 us

profile of v1, /device:TPU:0, one launch (start us, length us, event | category | flops | bytes accessed | tf_op | source)
XLA Modules:
  0.0 389.3 jit_solution(6919098052084498544)
XLA Ops:
  0.7 4.2 %multiply_reduce_fusion.2 = (f32[]{:T(128)}, f32[4096]{0:T(1024)S(1)}, f32[128]{0:T(128)S(1)}) fusion(f32[128,4096]{1,0:T(8,128)} %param.7, f32[4096]{0:T(1024)} %param.11, f32[128,4096]{1,0:T(8,128)} %param.6, f32[128]{0:T(128)} %param.10), kind=kLoop, calls=%fused_computation.6 | loop fusion | flops 5238655 | bytes 4228100 | tf_op jit(solution)/shard_map/reduce_sum | solution.py:25
  4.9 42.2 %psum.123 = f32[]{:T(128)} all-reduce(f32[]{:T(128)} %get-tuple-element.11), channel_id=1, replica_groups=mesh['wide'=8,'narrow'=4] {'wide','narrow'}, use_global_device_ids=true, to_apply=%region_9.0 | all-reduce | flops 1 | bytes 8 | tf_op jit(solution)/shard_map/psum | solution.py:34
  47.7 36.8 %psum.120 = f32[4096]{0:T(1024)S(1)} all-reduce(f32[4096]{0:T(1024)S(1)} %get-tuple-element.12), channel_id=1, replica_groups=mesh['wide'=8,'narrow'=4] {'wide'}, use_global_device_ids=true, to_apply=%region_4.0 | all-reduce | flops 4096 | bytes 32768 | tf_op jit(solution)/shard_map/psum | solution.py:30
  84.4 5.6 %psum.119 = f32[128]{0:T(128)S(1)} all-reduce(f32[128]{0:T(128)S(1)} %get-tuple-element.13), channel_id=1, replica_groups=mesh['wide'=8,'narrow'=4] {'narrow'}, use_global_device_ids=true, to_apply=%region_1.0 | all-reduce | flops 128 | bytes 1024 | tf_op jit(solution)/shard_map/psum | solution.py:26
  91.3 0.6 multiply_reduce_fusion.5
  92.6 6.7 %psum.121 = f32[]{:T(128)} all-reduce(f32[]{:T(128)S(6)} %add.100), channel_id=1, replica_groups=mesh['wide'=8,'narrow'=4] {'narrow'}, use_global_device_ids=true, to_apply=%region_6.0 | all-reduce | flops 1 | bytes 8 | tf_op jit(solution)/shard_map/psum | solution.py:38
  99.2 17.7 %psum.122 = f32[]{:T(128)} all-reduce(f32[]{:T(128)} %psum.121), channel_id=1, replica_groups=mesh['wide'=8,'narrow'=4] {'wide'}, use_global_device_ids=true, to_apply=%region_7.0 | all-reduce | flops 1 | bytes 8 | tf_op jit(solution)/shard_map/psum | solution.py:38
  117.8 3.7 multiply_reduce_fusion.1
  121.5 38.3 %psum.128 = f32[]{:T(128)} all-reduce(f32[]{:T(128)} %get-tuple-element.8), channel_id=1, replica_groups=mesh['wide'=8,'narrow'=4] {'wide','narrow'}, use_global_device_ids=true, to_apply=%region_19.0 | all-reduce | flops 1 | bytes 8 | tf_op jit(solution)/shard_map/psum | solution.py:34
  160.5 6.0 %psum.124 = f32[128]{0:T(128)S(1)} all-reduce(f32[128]{0:T(128)S(1)} %get-tuple-element.9), channel_id=1, replica_groups=mesh['wide'=8,'narrow'=4] {'narrow'}, use_global_device_ids=true, to_apply=%region_11.0 | all-reduce | flops 128 | bytes 1024 | tf_op jit(solution)/shard_map/psum | solution.py:26
  167.8 36.4 %psum.125 = f32[4096]{0:T(1024)S(1)} all-reduce(f32[4096]{0:T(1024)S(1)} %get-tuple-element.10), channel_id=1, replica_groups=mesh['wide'=8,'narrow'=4] {'wide'}, use_global_device_ids=true, to_apply=%region_14.0 | all-reduce | flops 4096 | bytes 32768 | tf_op jit(solution)/shard_map/psum | solution.py:30
  204.2 0.6 multiply_reduce_fusion.4
  205.4 6.2 %psum.126 = f32[]{:T(128)} all-reduce(f32[]{:T(128)S(6)} %add.106), channel_id=1, replica_groups=mesh['wide'=8,'narrow'=4] {'narrow'}, use_global_device_ids=true, to_apply=%region_16.0 | all-reduce | flops 1 | bytes 8 | tf_op jit(solution)/shard_map/psum | solution.py:38
  211.6 17.7 %psum.127 = f32[]{:T(128)} all-reduce(f32[]{:T(128)} %psum.126), channel_id=1, replica_groups=mesh['wide'=8,'narrow'=4] {'wide'}, use_global_device_ids=true, to_apply=%region_17.0 | all-reduce | flops 1 | bytes 8 | tf_op jit(solution)/shard_map/psum | solution.py:38
  230.2 4.2 %multiply_reduce_fusion = (f32[]{:T(128)}, f32[128]{0:T(128)S(1)}, f32[4096]{0:T(1024)S(1)}) fusion(f32[4096]{0:T(1024)S(1)} %get-tuple-element.20, f32[128,4096]{1,0:T(8,128)} %param.6, f32[128]{0:T(128)S(1)} %get-tuple-element.22, f32[]{:T(128)S(6)} %div.43, f32[4096]{0:T(1024)S(1)} %get-tuple-element.24, f32[128]{0:T(128)S(1)} %get-tuple-element.26, ...), kind=kLoop, calls=%fused_computation.2 | loop fusion | flops 10481535 | bytes 4261900 | tf_op jit(solution)/shard_map/reduce_sum | solution.py:25
  234.4 38.0 %psum.133 = f32[]{:T(128)} all-reduce(f32[]{:T(128)} %get-tuple-element.5), channel_id=1, replica_groups=mesh['wide'=8,'narrow'=4] {'wide','narrow'}, use_global_device_ids=true, to_apply=%region_29.0 | all-reduce | flops 1 | bytes 8 | tf_op jit(solution)/shard_map/psum | solution.py:34
  273.0 6.4 %psum.129 = f32[128]{0:T(128)S(1)} all-reduce(f32[128]{0:T(128)S(1)} %get-tuple-element.6), channel_id=1, replica_groups=mesh['wide'=8,'narrow'=4] {'narrow'}, use_global_device_ids=true, to_apply=%region_21.0 | all-reduce | flops 128 | bytes 1024 | tf_op jit(solution)/shard_map/psum | solution.py:26
  280.6 36.1 %psum.130 = f32[4096]{0:T(1024)S(1)} all-reduce(f32[4096]{0:T(1024)S(1)} %get-tuple-element.7), channel_id=1, replica_groups=mesh['wide'=8,'narrow'=4] {'wide'}, use_global_device_ids=true, to_apply=%region_24.0 | all-reduce | flops 4096 | bytes 32768 | tf_op jit(solution)/shard_map/psum | solution.py:30
  318.0 6.2 %psum.131 = f32[]{:T(128)} all-reduce(f32[]{:T(128)S(6)} %add.112), channel_id=1, replica_groups=mesh['wide'=8,'narrow'=4] {'narrow'}, use_global_device_ids=true, to_apply=%region_26.0 | all-reduce | flops 1 | bytes 8 | tf_op jit(solution)/shard_map/psum | solution.py:38
  324.2 17.7 %psum.132 = f32[]{:T(128)} all-reduce(f32[]{:T(128)} %psum.131), channel_id=1, replica_groups=mesh['wide'=8,'narrow'=4] {'wide'}, use_global_device_ids=true, to_apply=%region_27.0 | all-reduce | flops 1 | bytes 8 | tf_op jit(solution)/shard_map/psum | solution.py:38
  342.8 4.9 %fusion.6 = (f32[4096]{0:T(1024)S(1)}, f32[128]{0:T(128)S(1)}, f32[128,4096]{1,0:T(8,128)}) fusion(f32[4096]{0:T(1024)S(1)} %get-tuple-element.20, f32[128,4096]{1,0:T(8,128)} %param.6, f32[128]{0:T(128)S(1)} %get-tuple-element.22, f32[]{:T(128)S(6)} %div.43, f32[4096]{0:T(1024)S(1)} %get-tuple-element.24, f32[128]{0:T(128)S(1)} %get-tuple-element.26, ...), kind=kLoop, calls=%fused_computation.17 | loop fusion | flops 12054400 | bytes 6375948 | tf_op jit(solution)/shard_map/reduce_sum | solution.py:29
  347.7 34.9 %psum.135 = f32[4096]{0:T(1024)S(1)} all-reduce(f32[4096]{0:T(1024)S(1)} %get-tuple-element.3), channel_id=1, replica_groups=mesh['wide'=8,'narrow'=4] {'wide'}, use_global_device_ids=true, to_apply=%region_33.0 | all-reduce | flops 4096 | bytes 32768 | tf_op jit(solution)/shard_map/psum | solution.py:30
  382.6 0.6 multiply_add_fusion
  383.2 5.6 %psum.134 = f32[128]{0:T(128)S(1)} all-reduce(f32[128]{0:T(128)S(1)} %get-tuple-element.4), channel_id=1, replica_groups=mesh['wide'=8,'narrow'=4] {'narrow'}, use_global_device_ids=true, to_apply=%region_31.0 | all-reduce | flops 128 | bytes 1024 | tf_op jit(solution)/shard_map/psum | solution.py:26
  (15 shorter events, 3.0 us)
Async XLA Ops:
  0.6 90.7 %copy-start.1 = (f32[4096]{0:T(1024)S(1)}, f32[4096]{0:T(1024)}, u32[]{:S(2)}) copy-start(f32[4096]{0:T(1024)} %param.11) | copy-start | bytes 49156
  0.6 89.4 %copy-start.3 = (f32[128]{0:T(128)S(1)}, f32[128]{0:T(128)}, u32[]{:S(2)}) copy-start(f32[128]{0:T(128)} %param.10) | copy-start | bytes 1540
  0.7 90.7 %copy-start.2 = (f32[4096]{0:T(1024)S(1)}, f32[4096]{0:T(1024)}, u32[]{:S(2)}) copy-start(f32[4096]{0:T(1024)} %param.9) | copy-start | bytes 49156
  0.7 89.4 %copy-start.4 = (f32[128]{0:T(128)S(1)}, f32[128]{0:T(128)}, u32[]{:S(2)}) copy-start(f32[128]{0:T(128)} %param.8) | copy-start | bytes 1540
  0.7 117.1 %copy-start = (f32[128,4096]{1,0:T(8,128)S(1)}, f32[128,4096]{1,0:T(8,128)}, u32[]{:S(2)}) copy-start(f32[128,4096]{1,0:T(8,128)} %param.7) | copy-start | bytes 6291460
